TPU v7x, 32 devices: a whole 2x2x4 slice. The times are simulated.
32 devices in a mesh: depth: 2 (over y), lat: 16 (over z, x, core).
Axes of the slice: x: 2, y: 2, z: 4, core: 2. Of those that a mesh axis runs over, the one named last changes fastest.
Arguments:
- down_state: bfloat16 [2, 192, 32768], P('depth', None, 'lat'), may hold values from -6 to 6
- up_state: bfloat16 [2, 192, 32768], P('depth', None, 'lat'), may hold values from -6 to 6
- reflectivity: float32 [2, 32768], P('depth', 'lat'), may hold values from -0.3 to 0.3
- w_down: bfloat16 [2, 16, 2048, 1024], P('depth', 'lat'), may hold values from -0.125 to 0.125
- w_up: bfloat16 [2, 16, 2048, 1024], P('depth', 'lat'), may hold values from -0.125 to 0.125
Outputs:
- down_final: bfloat16 [2, 192, 32768], P('depth', None, 'lat')
- up_final: bfloat16 [2, 192, 32768], P('depth', None, 'lat')
All inputs are finite; a program needn't handle non-finite values.
Results may differ from a plain program's by a relative error of at most 0.0086.
Values may be sent and summed in bfloat16 or wider, within the bound.
A program may use at most 64 MiB of HBM per device.

v0:
```python
import functools

import jax
import jax.numpy as jnp
from jax import lax
from jax.experimental import pallas as pl
from jax.experimental.pallas import tpu as pltpu
from jax.sharding import PartitionSpec as P

BLOCK = 1024
HALO = 512
TICKS = 4
VMEM_BYTES = 67043328
MESH = pl.DeviceIdType.MESH


def chunks_of(columns):
    for count in (3, 2):
        if columns % (16 * count) == 0:
            return count
    return 1


def kernel(
    depths, lats, chunks,
    down_in, up_in, reflect_in, wd_in, wu_in,
    down_out, up_out,
    state, padded, outs, weights, reflect_ref,
    in_sem, w_sem, r_sem, halo_send, halo_recv, depth_send, depth_recv,
):
    level = lax.axis_index("depth")
    lat = lax.axis_index("lat")
    rows, points = state.shape[2], state.shape[3]
    steps = TICKS * chunks
    blocks = points // BLOCK
    not_first, not_last = level > 0, level < depths - 1
    has_left, has_right = lat > 0, lat < lats - 1
    neighbours = (
        (has_left, {"lat": lat - 1}),
        (has_right, {"lat": lat + 1}),
        (not_first, {"depth": level - 1}),
        (not_last, {"depth": level + 1}),
    )

    def in_copy(c, f):
        source = (down_in, up_in)[f]
        return pltpu.make_async_copy(
            source.at[0, pl.ds(c * rows, rows)], state.at[c, f], in_sem.at[c, f]
        )

    def w_copy(f):
        return pltpu.make_async_copy((wd_in, wu_in)[f].at[0, 0], weights.at[f], w_sem.at[f])

    def r_copy():
        return pltpu.make_async_copy(reflect_in, reflect_ref, r_sem)

    def halo_copy(k, side, f):
        source = HALO if side == 0 else points
        target = HALO + points if side == 0 else 0
        return pltpu.make_async_remote_copy(
            src_ref=padded.at[k, f, :, pl.ds(source, HALO)],
            dst_ref=padded.at[k, f, :, pl.ds(target, HALO)],
            send_sem=halo_send.at[k, side, f],
            recv_sem=halo_recv.at[k, side, f],
            device_id={"lat": lat - 1 if side == 0 else lat + 1},
            device_id_type=MESH,
        )

    def next_state(k, f, last):
        if last:
            start = pl.multiple_of((k - (steps - chunks)) * rows, rows)
            return (down_out, up_out)[f].at[0, pl.ds(start, rows)]
        return state.at[k + chunks, f]

    def depth_copy(k, f, last):
        return pltpu.make_async_remote_copy(
            src_ref=outs.at[k, f],
            dst_ref=next_state(k, f, last),
            send_sem=depth_send.at[k, f],
            recv_sem=depth_recv.at[k, f],
            device_id={"depth": level + 1 if f == 0 else level - 1},
            device_id_type=MESH,
        )

    def in_turn(turn):
        return lax.rem(turn + (level == depths - 1).astype(jnp.int32), 2)

    for f in range(2):
        in_copy(0, f).start()
    r_copy().start()

    barrier = pltpu.get_barrier_semaphore()
    for present, device in neighbours:
        @pl.when(present)
        def _():
            pl.semaphore_signal(barrier, inc=1, device_id=device, device_id_type=MESH)

    for c in range(1, chunks):
        for f in range(2):
            in_copy(c, f).start()

    def arrived(k, last):
        @pl.when(not_first)
        def _():
            depth_copy(k, 0, last).wait_recv()

        @pl.when(not_last)
        def _():
            depth_copy(k, 1, last).wait_recv()

    def mix(k):
        @pl.loop(0, 2)
        def _(turn):
            f = in_turn(turn)
            reflect = jnp.where(f == 0, 1.0, -1.0) * reflect_ref[...]
            own = state[k, f].astype(jnp.float32)
            other = state[k, 1 - f].astype(jnp.float32)
            padded[k, f, :, HALO : HALO + points] = (
                (1.0 + reflect) * own - reflect * other
            ).astype(jnp.bfloat16)

            @pl.when(has_left)
            def _():
                halo_copy(k, 0, f).start()

            @pl.when(has_right)
            def _():
                halo_copy(k, 1, f).start()

    def extrapolate(k, last, first=False):
        @pl.loop(0, 2)
        def _(turn):
            f = in_turn(turn)
            if first:
                for g in range(2):
                    @pl.when(f == g)
                    def _():
                        w_copy(g).wait()

            @pl.when(has_right)
            def _():
                halo_copy(k, 0, f).wait_recv()

            @pl.when(has_left)
            def _():
                halo_copy(k, 1, f).wait_recv()

            windows = jnp.concatenate(
                [padded[k, f, :, b * BLOCK : b * BLOCK + BLOCK + 2 * HALO] for b in range(blocks)],
                axis=0,
            )
            summed = jnp.dot(windows, weights[f], preferred_element_type=jnp.float32)
            summed = summed.astype(jnp.bfloat16)
            for b in range(blocks):
                outs[k, f, :, b * BLOCK : (b + 1) * BLOCK] = summed[b * rows : (b + 1) * rows]

            @pl.when((f == 0) & not_last)
            def _():
                depth_copy(k, 0, last).start()

            @pl.when((f == 1) & not_first)
            def _():
                depth_copy(k, 1, last).start()

            @pl.when((f == 1) & (level == 0))
            def _():
                next_state(k, 0, last)[...] = -outs[k, 1]

            @pl.when((f == 1) & (level == depths - 1))
            def _():
                next_state(k, 1, last)[...] = jnp.zeros((rows, points), jnp.bfloat16)

    for f in range(2):
        in_copy(0, f).wait()
    r_copy().wait()
    for turn in range(2):
        for f in range(2):
            @pl.when(in_turn(turn) == f)
            def _():
                w_copy(f).start()
    pl.semaphore_wait(barrier, sum(present.astype(jnp.int32) for present, _ in neighbours))
    mix(0)

    zero_rim = jnp.zeros((2, rows, HALO), jnp.bfloat16)

    @pl.when(lat == 0)
    def _():
        @pl.loop(0, steps)
        def _(k):
            padded[k, :, :, :HALO] = zero_rim

    @pl.when(lat == lats - 1)
    def _():
        @pl.loop(0, steps)
        def _(k):
            padded[k, :, :, HALO + points :] = zero_rim

    for c in range(1, chunks):
        for f in range(2):
            in_copy(c, f).wait()

    @pl.loop(1, chunks)
    def _(k):
        mix(k)

    extrapolate(0, False, True)

    @pl.loop(1, chunks - 1)
    def _(k):
        extrapolate(k, False)

    @pl.loop(chunks, steps - chunks + 1)
    def _(k):
        arrived(k - chunks, False)
        mix(k)
        extrapolate(k - 1, False)

    @pl.loop(steps - chunks + 1, steps)
    def _(k):
        arrived(k - chunks, False)
        mix(k)
        extrapolate(k - 1, True)

    extrapolate(steps - 1, True)

    def sent(k, last):
        for f in range(2):
            @pl.when(has_left)
            def _():
                halo_copy(k, 0, f).wait_send()

            @pl.when(has_right)
            def _():
                halo_copy(k, 1, f).wait_send()

        @pl.when(not_last)
        def _():
            depth_copy(k, 0, last).wait_send()

        @pl.when(not_first)
        def _():
            depth_copy(k, 1, last).wait_send()

    @pl.loop(0, steps - chunks)
    def _(k):
        sent(k, False)

    @pl.loop(steps - chunks, steps)
    def _(k):
        sent(k, True)
        arrived(k, True)


def solution(mesh):
    depths, lats = mesh.shape["depth"], mesh.shape["lat"]

    def on_device(down_state, up_state, reflectivity, w_down, w_up):
        _, columns, points = down_state.shape
        chunks = chunks_of(columns)
        rows = columns // chunks
        steps = TICKS * chunks
        window = w_down.shape[2]
        field = pltpu.VMEM(down_state.shape, jnp.bfloat16)
        landing = pl.BlockSpec(memory_space=pltpu.VMEM)
        anywhere = pl.BlockSpec(memory_space=pl.ANY)
        flops = 2 * 2 * TICKS * columns * points * window
        return pl.pallas_call(
            functools.partial(kernel, depths, lats, chunks),
            out_shape=(field, field),
            in_specs=[anywhere] * 5,
            out_specs=(landing, landing),
            scratch_shapes=[
                pltpu.VMEM((steps, 2, rows, points), jnp.bfloat16),
                pltpu.VMEM((steps, 2, rows, points + 2 * HALO), jnp.bfloat16),
                pltpu.VMEM((steps, 2, rows, points), jnp.bfloat16),
                pltpu.VMEM((2, window, BLOCK), jnp.bfloat16),
                pltpu.VMEM((1, points), jnp.float32),
                pltpu.SemaphoreType.DMA((chunks, 2)),
                pltpu.SemaphoreType.DMA((2,)),
                pltpu.SemaphoreType.DMA,
                pltpu.SemaphoreType.DMA((steps, 2, 2)),
                pltpu.SemaphoreType.DMA((steps, 2, 2)),
                pltpu.SemaphoreType.DMA((steps, 2)),
                pltpu.SemaphoreType.DMA((steps, 2)),
            ],
            compiler_params=pltpu.CompilerParams(
                collective_id=0, has_side_effects=True, vmem_limit_bytes=VMEM_BYTES - 2 * 2 * down_state.size
            ),
            cost_estimate=pl.CostEstimate(
                flops=flops, bytes_accessed=4 * w_down.size * 2, transcendentals=0
            ),
        )(down_state, up_state, reflectivity, w_down, w_up)

    in_specs = (
        P("depth", None, "lat"),
        P("depth", None, "lat"),
        P("depth", "lat"),
        P("depth", "lat", None, None),
        P("depth", "lat", None, None),
    )
    out_specs = (P("depth", None, "lat"), P("depth", None, "lat"))
    return jax.shard_map(
        on_device, mesh=mesh, in_specs=in_specs, out_specs=out_specs, check_vma=False
    )
```

profile of v0, /device:TPU:0, one launch (start us, length us, event | category | flops | bytes accessed | tf_op | source)
XLA Modules:
  0.0 79.0 jit_solution(7613772779016407243)
XLA Ops:
  0.6 76.6 %shard_map.68 = (bf16[1,192,2048]{2,1,0:T(8,128)(2,1)S(1)}, bf16[1,192,2048]{2,1,0:T(8,128)(2,1)S(1)}) custom-call(bf16[1,192,2048]{2,1,0:T(8,128)(2,1)} %down_in.1, bf16[1,192,2048]{2,1,0:T(8,128)(2,1)} %up_in.1, f32[1,2048]{1,0:T(1,128)} %reflect_in.1, bf16[1,1,2048,1024]{3,2,1,0:T(8,128)(2,1)} %wd_in.1, bf16[1,1,2048,1024]{3,2,1,0:T(8,128)(2,1)} %wu_in.1), custom_call_target="tpu_custom_call" | custom-call | flops 12884901888 | bytes 16777216 | tf_op jit(solution)/shard_map/pallas_call | solution.py:267
  77.3 0.9 %copy.9 = bf16[1,192,2048]{2,1,0:T(8,128)(2,1)} copy(bf16[1,192,2048]{2,1,0:T(8,128)(2,1)S(1)} %get-tuple-element.2) | data formatting | bytes 1572864
  78.1 0.9 %copy.10 = bf16[1,192,2048]{2,1,0:T(8,128)(2,1)} copy(bf16[1,192,2048]{2,1,0:T(8,128)(2,1)S(1)} %get-tuple-element.3) | data formatting | bytes 1572864
where the time goes:
time: 79.9 us; the launch traced here: 79 us
  Pallas kernels  76.6 us (96%)
  local copies, waits for them, and re-layouts  1.76 us (2%)
    pallas_call x1, Pallas kernels, on_device(): pl.pallas_call(functools.partial(kernel, depths, lats, chunks), out_shape...  76.6 us
    unnamed x2, local copies, waits for them, and re-layouts  1.76 us

commit v1 on v0

--- a/solution.py
+++ b/solution.py
@@ -10,6 +10,8 @@
 BLOCK = 1024
 HALO = 512
 TICKS = 4
+SLICE = 256
+SLICES = BLOCK // SLICE
 VMEM_BYTES = 67043328
 MESH = pl.DeviceIdType.MESH
 
@@ -48,8 +50,17 @@
             source.at[0, pl.ds(c * rows, rows)], state.at[c, f], in_sem.at[c, f]
         )
 
-    def w_copy(f):
-        return pltpu.make_async_copy((wd_in, wu_in)[f].at[0, 0], weights.at[f], w_sem.at[f])
+    def w_copy(f, n):
+        columns = pl.ds(pl.multiple_of(n * SLICE, SLICE), SLICE)
+        return pltpu.make_async_copy(
+            (wd_in, wu_in)[f].at[0, 0, :, columns], weights.at[f, :, columns], w_sem.at[f, n]
+        )
+
+    def weights_wait(f, n):
+        for g in range(2):
+            @pl.when(f == g)
+            def _():
+                w_copy(g, n).wait()
 
     def r_copy():
         return pltpu.make_async_copy(reflect_in, reflect_ref, r_sem)
@@ -82,22 +93,34 @@
             device_id_type=MESH,
         )
 
+    def depth_slice(k, f, start):
+        columns = pl.ds(start, SLICE)
+        return pltpu.make_async_remote_copy(
+            src_ref=outs.at[k, f, :, columns],
+            dst_ref=next_state(k, f, False).at[:, columns],
+            send_sem=depth_send.at[k, f],
+            recv_sem=depth_recv.at[k, f],
+            device_id={"depth": level + 1 if f == 0 else level - 1},
+            device_id_type=MESH,
+        )
+
     def in_turn(turn):
         return lax.rem(turn + (level == depths - 1).astype(jnp.int32), 2)
+
+    barrier = pltpu.get_barrier_semaphore()
+    for present, device in neighbours:
+        @pl.when(present)
+        def _():
+            pl.semaphore_signal(barrier, inc=1, device_id=device, device_id_type=MESH)
 
     for f in range(2):
         in_copy(0, f).start()
     r_copy().start()
-
-    barrier = pltpu.get_barrier_semaphore()
-    for present, device in neighbours:
-        @pl.when(present)
-        def _():
-            pl.semaphore_signal(barrier, inc=1, device_id=device, device_id_type=MESH)
-
-    for c in range(1, chunks):
-        for f in range(2):
-            in_copy(c, f).start()
+    def weights_start(f, n):
+        for g in range(2):
+            @pl.when(f == g)
+            def _():
+                w_copy(g, n).start()
 
     def arrived(k, last):
         @pl.when(not_first)
@@ -107,79 +130,106 @@
         @pl.when(not_last)
         def _():
             depth_copy(k, 1, last).wait_recv()
+
+    def mix_field(k, f):
+        reflect = jnp.where(f == 0, 1.0, -1.0) * reflect_ref[...]
+        own = state[k, f].astype(jnp.float32)
+        other = state[k, 1 - f].astype(jnp.float32)
+        padded[k, f, :, HALO : HALO + points] = (
+            (1.0 + reflect) * own - reflect * other
+        ).astype(jnp.bfloat16)
+
+    def send_halo(k, f):
+        @pl.when(has_left)
+        def _():
+            halo_copy(k, 0, f).start()
+
+        @pl.when(has_right)
+        def _():
+            halo_copy(k, 1, f).start()
 
     def mix(k):
         @pl.loop(0, 2)
         def _(turn):
             f = in_turn(turn)
-            reflect = jnp.where(f == 0, 1.0, -1.0) * reflect_ref[...]
-            own = state[k, f].astype(jnp.float32)
-            other = state[k, 1 - f].astype(jnp.float32)
-            padded[k, f, :, HALO : HALO + points] = (
-                (1.0 + reflect) * own - reflect * other
+            mix_field(k, f)
+            send_halo(k, f)
+
+    def finish(k, f, last):
+        @pl.when((f == 1) & (level == 0))
+        def _():
+            next_state(k, 0, last)[...] = -outs[k, 1]
+
+        @pl.when((f == 1) & (level == depths - 1))
+        def _():
+            next_state(k, 1, last)[...] = jnp.zeros((rows, points), jnp.bfloat16)
+
+    def first_block(f, b):
+        rim = b == blocks - 1
+
+        @pl.when(rim & has_right)
+        def _():
+            halo_copy(0, 0, f).wait_recv()
+
+        @pl.when((b == 0) & has_left)
+        def _():
+            halo_copy(0, 1, f).wait_recv()
+
+        @pl.loop(0, SLICES)
+        def _(n):
+            @pl.when(b == near)
+            def _():
+                weights_wait(f, n)
+
+            base = pl.multiple_of(b * BLOCK, BLOCK)
+            start = pl.multiple_of(base + n * SLICE, SLICE)
+            columns = pl.ds(pl.multiple_of(n * SLICE, SLICE), SLICE)
+            outs[0, f, :, pl.ds(start, SLICE)] = jnp.dot(
+                padded[0, f, :, pl.ds(base, BLOCK + 2 * HALO)],
+                weights[f, :, columns],
+                preferred_element_type=jnp.float32,
             ).astype(jnp.bfloat16)
 
-            @pl.when(has_left)
-            def _():
-                halo_copy(k, 0, f).start()
-
-            @pl.when(has_right)
-            def _():
-                halo_copy(k, 1, f).start()
-
-    def extrapolate(k, last, first=False):
+            @pl.when((f == 0) & not_last)
+            def _():
+                depth_slice(0, 0, start).start()
+
+            @pl.when((f == 1) & not_first)
+            def _():
+                depth_slice(0, 1, start).start()
+
+    def extrapolate_field(k, f, last):
+        @pl.when(has_right)
+        def _():
+            halo_copy(k, 0, f).wait_recv()
+
+        @pl.when(has_left)
+        def _():
+            halo_copy(k, 1, f).wait_recv()
+
+        windows = jnp.concatenate(
+            [padded[k, f, :, b * BLOCK : b * BLOCK + BLOCK + 2 * HALO] for b in range(blocks)],
+            axis=0,
+        )
+        summed = jnp.dot(windows, weights[f], preferred_element_type=jnp.float32)
+        summed = summed.astype(jnp.bfloat16)
+        for b in range(blocks):
+            outs[k, f, :, b * BLOCK : (b + 1) * BLOCK] = summed[b * rows : (b + 1) * rows]
+
+        @pl.when((f == 0) & not_last)
+        def _():
+            depth_copy(k, 0, last).start()
+
+        @pl.when((f == 1) & not_first)
+        def _():
+            depth_copy(k, 1, last).start()
+
+        finish(k, f, last)
+
+    def extrapolate(k, last):
         @pl.loop(0, 2)
         def _(turn):
-            f = in_turn(turn)
-            if first:
-                for g in range(2):
-                    @pl.when(f == g)
-                    def _():
-                        w_copy(g).wait()
-
-            @pl.when(has_right)
-            def _():
-                halo_copy(k, 0, f).wait_recv()
-
-            @pl.when(has_left)
-            def _():
-                halo_copy(k, 1, f).wait_recv()
-
-            windows = jnp.concatenate(
-                [padded[k, f, :, b * BLOCK : b * BLOCK + BLOCK + 2 * HALO] for b in range(blocks)],
-                axis=0,
-            )
-            summed = jnp.dot(windows, weights[f], preferred_element_type=jnp.float32)
-            summed = summed.astype(jnp.bfloat16)
-            for b in range(blocks):
-                outs[k, f, :, b * BLOCK : (b + 1) * BLOCK] = summed[b * rows : (b + 1) * rows]
-
-            @pl.when((f == 0) & not_last)
-            def _():
-                depth_copy(k, 0, last).start()
-
-            @pl.when((f == 1) & not_first)
-            def _():
-                depth_copy(k, 1, last).start()
-
-            @pl.when((f == 1) & (level == 0))
-            def _():
-                next_state(k, 0, last)[...] = -outs[k, 1]
-
-            @pl.when((f == 1) & (level == depths - 1))
-            def _():
-                next_state(k, 1, last)[...] = jnp.zeros((rows, points), jnp.bfloat16)
-
-    for f in range(2):
-        in_copy(0, f).wait()
-    r_copy().wait()
-    for turn in range(2):
-        for f in range(2):
-            @pl.when(in_turn(turn) == f)
-            def _():
-                w_copy(f).start()
-    pl.semaphore_wait(barrier, sum(present.astype(jnp.int32) for present, _ in neighbours))
-    mix(0)
+            extrapolate_field(k, in_turn(turn), last)
 
     zero_rim = jnp.zeros((2, rows, HALO), jnp.bfloat16)
 
@@ -195,15 +245,45 @@
         def _(k):
             padded[k, :, :, HALO + points :] = zero_rim
 
-    for c in range(1, chunks):
+    early, late = in_turn(0), in_turn(1)
+    near = lax.rem(lat + 1, 2)
+    for f in range(2):
+        in_copy(0, f).wait()
+    r_copy().wait()
+    weights_start(early, 0)
+    weights_start(early, 1)
+    mix_field(0, early)
+    pl.semaphore_wait(barrier, sum(present.astype(jnp.int32) for present, _ in neighbours))
+    send_halo(0, early)
+    for n in range(2, SLICES):
+        weights_start(early, n)
+    mix_field(0, late)
+    send_halo(0, late)
+    for f in range(2):
+        in_copy(1, f).start()
+
+    first_block(early, near)
+    for n in range(SLICES):
+        weights_start(late, n)
+    for c in range(2, chunks):
+        for f in range(2):
+            in_copy(c, f).start()
+    for f in range(2):
+        in_copy(1, f).wait()
+    mix(1)
+    first_block(early, 1 - near)
+    finish(0, early, False)
+    for n in range(SLICES):
+        weights_wait(late, n)
+    extrapolate_field(0, late, False)
+
+    for c in range(2, chunks):
         for f in range(2):
             in_copy(c, f).wait()
 
-    @pl.loop(1, chunks)
+    @pl.loop(2, chunks)
     def _(k):
         mix(k)
-
-    extrapolate(0, False, True)
 
     @pl.loop(1, chunks - 1)
     def _(k):
@@ -276,7 +356,7 @@
                 pltpu.VMEM((2, window, BLOCK), jnp.bfloat16),
                 pltpu.VMEM((1, points), jnp.float32),
                 pltpu.SemaphoreType.DMA((chunks, 2)),
-                pltpu.SemaphoreType.DMA((2,)),
+                pltpu.SemaphoreType.DMA((2, SLICES)),
                 pltpu.SemaphoreType.DMA,
                 pltpu.SemaphoreType.DMA((steps, 2, 2)),
                 pltpu.SemaphoreType.DMA((steps, 2, 2)),

time: 79.9 us -> 77.9 us (0.975)
  Pallas kernels: 76.6 us -> 75.4 us
    pallas_call x1, Pallas kernels: 76.6 us -> 75.4 us  [on_device(): pl.pallas_call(functools.partial(kernel, depths, lats, chunks), out_shape...]
where the time goes in v1:
time: 77.9 us; the launch traced here: 77.8 us
  Pallas kernels  75.4 us (97%)
  local copies, waits for them, and re-layouts  1.76 us (2%)
    pallas_call x1, Pallas kernels, on_device(): pl.pallas_call(functools.partial(kernel, depths, lats, chunks), out_shape...  75.4 us
    unnamed x2, local copies, waits for them, and re-layouts  1.76 us

profile of v1, /device:TPU:0, one launch (start us, length us, event | category | flops | bytes accessed | tf_op | source)
XLA Modules:
  0.0 77.8 jit_solution(12611593410944811371)
XLA Ops:
  0.6 75.4 %shard_map.68 = (bf16[1,192,2048]{2,1,0:T(8,128)(2,1)S(1)}, bf16[1,192,2048]{2,1,0:T(8,128)(2,1)S(1)}) custom-call(bf16[1,192,2048]{2,1,0:T(8,128)(2,1)} %down_in.1, bf16[1,192,2048]{2,1,0:T(8,128)(2,1)} %up_in.1, f32[1,2048]{1,0:T(1,128)} %reflect_in.1, bf16[1,1,2048,1024]{3,2,1,0:T(8,128)(2,1)} %wd_in.1, bf16[1,1,2048,1024]{3,2,1,0:T(8,128)(2,1)} %wu_in.1), custom_call_target="tpu_custom_call" | custom-call | flops 12884901888 | bytes 16777216 | tf_op jit(solution)/shard_map/pallas_call | solution.py:347
  76.0 0.9 %copy.9 = bf16[1,192,2048]{2,1,0:T(8,128)(2,1)} copy(bf16[1,192,2048]{2,1,0:T(8,128)(2,1)S(1)} %get-tuple-element.2) | data formatting | bytes 1572864
  76.9 0.9 %copy.10 = bf16[1,192,2048]{2,1,0:T(8,128)(2,1)} copy(bf16[1,192,2048]{2,1,0:T(8,128)(2,1)S(1)} %get-tuple-element.3) | data formatting | bytes 1572864

commit v2 on v1

--- a/solution.py
+++ b/solution.py
@@ -113,14 +113,17 @@
         def _():
             pl.semaphore_signal(barrier, inc=1, device_id=device, device_id_type=MESH)
 
-    for f in range(2):
-        in_copy(0, f).start()
+    for c in range(2):
+        for f in range(2):
+            in_copy(c, f).start()
     r_copy().start()
     def weights_start(f, n):
         for g in range(2):
             @pl.when(f == g)
             def _():
                 w_copy(g, n).start()
+
+    weights_start(in_turn(0), 0)
 
     def arrived(k, last):
         @pl.when(not_first)
@@ -247,47 +250,56 @@
 
     early, late = in_turn(0), in_turn(1)
     near = lax.rem(lat + 1, 2)
-    for f in range(2):
-        in_copy(0, f).wait()
+
+    def prepare(k, f):
+        mix_field(k, f)
+        send_halo(k, f)
+
+    def inputs_start(c):
+        for f in range(2):
+            in_copy(c, f).start()
+
+    def inputs_wait(c):
+        for f in range(2):
+            in_copy(c, f).wait()
+
+    inputs_wait(0)
     r_copy().wait()
-    weights_start(early, 0)
     weights_start(early, 1)
     mix_field(0, early)
     pl.semaphore_wait(barrier, sum(present.astype(jnp.int32) for present, _ in neighbours))
     send_halo(0, early)
     for n in range(2, SLICES):
         weights_start(early, n)
-    mix_field(0, late)
-    send_halo(0, late)
-    for f in range(2):
-        in_copy(1, f).start()
-
+    prepare(0, late)
+    for c in range(2, chunks):
+        inputs_start(c)
     first_block(early, near)
     for n in range(SLICES):
         weights_start(late, n)
+    inputs_wait(1)
+    prepare(1, early)
+    prepare(1, late)
     for c in range(2, chunks):
-        for f in range(2):
-            in_copy(c, f).start()
-    for f in range(2):
-        in_copy(1, f).wait()
-    mix(1)
+        inputs_wait(c)
+
+    @pl.loop(2, chunks)
+    def _(k):
+        mix(k)
+
     first_block(early, 1 - near)
     finish(0, early, False)
+
+    @pl.loop(1, chunks - 1)
+    def _(k):
+        extrapolate_field(k, early, False)
+
     for n in range(SLICES):
         weights_wait(late, n)
-    extrapolate_field(0, late, False)
-
-    for c in range(2, chunks):
-        for f in range(2):
-            in_copy(c, f).wait()
-
-    @pl.loop(2, chunks)
-    def _(k):
-        mix(k)
-
-    @pl.loop(1, chunks - 1)
-    def _(k):
-        extrapolate(k, False)
+
+    @pl.loop(0, chunks - 1)
+    def _(k):
+        extrapolate_field(k, late, False)
 
     @pl.loop(chunks, steps - chunks + 1)
     def _(k):
@@ -329,6 +341,17 @@
     def _(k):
         sent(k, True)
         arrived(k, True)
+
+
+def store(down, up, down_out, up_out, sem):
+    copies = [
+        pltpu.make_async_copy(source, target, sem.at[f])
+        for f, (source, target) in enumerate(((down, down_out), (up, up_out)))
+    ]
+    for copy in copies:
+        copy.start()
+    for copy in copies:
+        copy.wait()
 
 
 def solution(mesh):
@@ -344,7 +367,7 @@
         landing = pl.BlockSpec(memory_space=pltpu.VMEM)
         anywhere = pl.BlockSpec(memory_space=pl.ANY)
         flops = 2 * 2 * TICKS * columns * points * window
-        return pl.pallas_call(
+        results = pl.pallas_call(
             functools.partial(kernel, depths, lats, chunks),
             out_shape=(field, field),
             in_specs=[anywhere] * 5,
@@ -370,6 +393,18 @@
                 flops=flops, bytes_accessed=4 * w_down.size * 2, transcendentals=0
             ),
         )(down_state, up_state, reflectivity, w_down, w_up)
+        results = [pltpu.with_memory_space_constraint(result, pltpu.VMEM) for result in results]
+        whole = jax.ShapeDtypeStruct(down_state.shape, jnp.bfloat16)
+        return pl.pallas_call(
+            store,
+            out_shape=(whole, whole),
+            in_specs=[landing] * 2,
+            out_specs=(anywhere, anywhere),
+            scratch_shapes=[pltpu.SemaphoreType.DMA((2,))],
+            cost_estimate=pl.CostEstimate(
+                flops=0, bytes_accessed=4 * 2 * down_state.size, transcendentals=0
+            ),
+        )(*results)
 
     in_specs = (
         P("depth", None, "lat"),

time: 77.9 us -> 77.4 us (level)
  local copies, waits for them, and re-layouts: 1.76 us -> 0 us
  Pallas kernels: 75.4 us -> 76.5 us
    unnamed x2 -> x0, local copies, waits for them, and re-layouts: 1.76 us -> none
    pallas_call x0 -> x1, Pallas kernels: none -> 1.16 us  [on_device(): pl.pallas_call(store, out_shape=(whole, whole), in_specs=[landing] * 2, o...]
where the time goes in v2:
time: 77.4 us; the launch traced here: 77.2 us
  Pallas kernels  76.5 us (99%)
    pallas_call x1, Pallas kernels, on_device(): pl.pallas_call(functools.partial(kernel, depths, lats, chunks), out_shape...  75.4 us

profile of v2, /device:TPU:0, one launch (start us, length us, event | category | flops | bytes accessed | tf_op | source)
XLA Modules:
  0.0 77.2 jit_solution(11399124317688689907)
XLA Ops:
  0.6 75.4 %shard_map.68 = (bf16[1,192,2048]{2,1,0:T(8,128)(2,1)S(1)}, bf16[1,192,2048]{2,1,0:T(8,128)(2,1)S(1)}) custom-call(bf16[1,192,2048]{2,1,0:T(8,128)(2,1)} %down_in.1, bf16[1,192,2048]{2,1,0:T(8,128)(2,1)} %up_in.1, f32[1,2048]{1,0:T(1,128)} %reflect_in.1, bf16[1,1,2048,1024]{3,2,1,0:T(8,128)(2,1)} %wd_in.1, bf16[1,1,2048,1024]{3,2,1,0:T(8,128)(2,1)} %wu_in.1), custom_call_target="tpu_custom_call" | custom-call | flops 12884901888 | bytes 16777216 | tf_op jit(solution)/shard_map/pallas_call | solution.py:370
  76.0 1.2 %shard_map.69 = (bf16[1,192,2048]{2,1,0:T(8,128)(2,1)}, bf16[1,192,2048]{2,1,0:T(8,128)(2,1)}) custom-call(bf16[1,192,2048]{2,1,0:T(8,128)(2,1)S(1)} %get-tuple-element.4.down, bf16[1,192,2048]{2,1,0:T(8,128)(2,1)S(1)} %get-tuple-element.5.up), custom_call_target="tpu_custom_call" | custom-call | bytes 3145728 | tf_op jit(solution)/shard_map/pallas_call | solution.py:398

commit v3 on v2

--- a/solution.py
+++ b/solution.py
@@ -34,6 +34,7 @@
     lat = lax.axis_index("lat")
     rows, points = state.shape[2], state.shape[3]
     steps = TICKS * chunks
+    ring = 2 * chunks
     blocks = points // BLOCK
     not_first, not_last = level > 0, level < depths - 1
     has_left, has_right = lat > 0, lat < lats - 1
@@ -44,6 +45,9 @@
         (not_last, {"depth": level + 1}),
     )
 
+    def slot(k):
+        return k % ring if isinstance(k, int) else lax.rem(k, ring)
+
     def in_copy(c, f):
         source = (down_in, up_in)[f]
         return pltpu.make_async_copy(
@@ -71,8 +75,8 @@
         return pltpu.make_async_remote_copy(
             src_ref=padded.at[k, f, :, pl.ds(source, HALO)],
             dst_ref=padded.at[k, f, :, pl.ds(target, HALO)],
-            send_sem=halo_send.at[k, side, f],
-            recv_sem=halo_recv.at[k, side, f],
+            send_sem=halo_send.at[slot(k), side, f],
+            recv_sem=halo_recv.at[slot(k), side, f],
             device_id={"lat": lat - 1 if side == 0 else lat + 1},
             device_id_type=MESH,
         )
@@ -87,8 +91,8 @@
         return pltpu.make_async_remote_copy(
             src_ref=outs.at[k, f],
             dst_ref=next_state(k, f, last),
-            send_sem=depth_send.at[k, f],
-            recv_sem=depth_recv.at[k, f],
+            send_sem=depth_send.at[slot(k), f],
+            recv_sem=depth_recv.at[slot(k), f],
             device_id={"depth": level + 1 if f == 0 else level - 1},
             device_id_type=MESH,
         )
@@ -98,8 +102,8 @@
         return pltpu.make_async_remote_copy(
             src_ref=outs.at[k, f, :, columns],
             dst_ref=next_state(k, f, False).at[:, columns],
-            send_sem=depth_send.at[k, f],
-            recv_sem=depth_recv.at[k, f],
+            send_sem=depth_send.at[slot(k), f],
+            recv_sem=depth_recv.at[slot(k), f],
             device_id={"depth": level + 1 if f == 0 else level - 1},
             device_id_type=MESH,
         )
@@ -301,20 +305,6 @@
     def _(k):
         extrapolate_field(k, late, False)
 
-    @pl.loop(chunks, steps - chunks + 1)
-    def _(k):
-        arrived(k - chunks, False)
-        mix(k)
-        extrapolate(k - 1, False)
-
-    @pl.loop(steps - chunks + 1, steps)
-    def _(k):
-        arrived(k - chunks, False)
-        mix(k)
-        extrapolate(k - 1, True)
-
-    extrapolate(steps - 1, True)
-
     def sent(k, last):
         for f in range(2):
             @pl.when(has_left)
@@ -333,7 +323,27 @@
         def _():
             depth_copy(k, 1, last).wait_send()
 
-    @pl.loop(0, steps - chunks)
+    @pl.loop(chunks, steps - chunks + 1)
+    def _(k):
+        arrived(k - chunks, False)
+
+        @pl.when(k >= ring)
+        def _():
+            sent(k - ring, False)
+
+        mix(k)
+        extrapolate(k - 1, False)
+
+    @pl.loop(steps - chunks + 1, steps)
+    def _(k):
+        arrived(k - chunks, False)
+        sent(k - ring, False)
+        mix(k)
+        extrapolate(k - 1, True)
+
+    extrapolate(steps - 1, True)
+
+    @pl.loop(steps - ring, steps - chunks)
     def _(k):
         sent(k, False)
 
@@ -381,10 +391,10 @@
                 pltpu.SemaphoreType.DMA((chunks, 2)),
                 pltpu.SemaphoreType.DMA((2, SLICES)),
                 pltpu.SemaphoreType.DMA,
-                pltpu.SemaphoreType.DMA((steps, 2, 2)),
-                pltpu.SemaphoreType.DMA((steps, 2, 2)),
-                pltpu.SemaphoreType.DMA((steps, 2)),
-                pltpu.SemaphoreType.DMA((steps, 2)),
+                pltpu.SemaphoreType.DMA((2 * chunks, 2, 2)),
+                pltpu.SemaphoreType.DMA((2 * chunks, 2, 2)),
+                pltpu.SemaphoreType.DMA((2 * chunks, 2)),
+                pltpu.SemaphoreType.DMA((2 * chunks, 2)),
             ],
             compiler_params=pltpu.CompilerParams(
                 collective_id=0, has_side_effects=True, vmem_limit_bytes=VMEM_BYTES - 2 * 2 * down_state.size

time: 77.4 us -> 76.7 us (level)
  no operation moved by 1% of the time
where the time goes in v3:
time: 76.7 us; the launch traced here: 76.5 us
  Pallas kernels  75.9 us (99%)
    pallas_call x1, Pallas kernels, on_device(): pl.pallas_call(functools.partial(kernel, depths, lats, chunks), out_shape...  74.7 us

profile of v3, /device:TPU:0, one launch (start us, length us, event | category | flops | bytes accessed | tf_op | source)
XLA Modules:
  0.0 76.5 jit_solution(6689907161019479377)
XLA Ops:
  0.6 74.7 %shard_map.68 = (bf16[1,192,2048]{2,1,0:T(8,128)(2,1)S(1)}, bf16[1,192,2048]{2,1,0:T(8,128)(2,1)S(1)}) custom-call(bf16[1,192,2048]{2,1,0:T(8,128)(2,1)} %down_in.1, bf16[1,192,2048]{2,1,0:T(8,128)(2,1)} %up_in.1, f32[1,2048]{1,0:T(1,128)} %reflect_in.1, bf16[1,1,2048,1024]{3,2,1,0:T(8,128)(2,1)} %wd_in.1, bf16[1,1,2048,1024]{3,2,1,0:T(8,128)(2,1)} %wu_in.1), custom_call_target="tpu_custom_call" | custom-call | flops 12884901888 | bytes 16777216 | tf_op jit(solution)/shard_map/pallas_call | solution.py:380
  75.4 1.2 %shard_map.69 = (bf16[1,192,2048]{2,1,0:T(8,128)(2,1)}, bf16[1,192,2048]{2,1,0:T(8,128)(2,1)}) custom-call(bf16[1,192,2048]{2,1,0:T(8,128)(2,1)S(1)} %get-tuple-element.4.down, bf16[1,192,2048]{2,1,0:T(8,128)(2,1)S(1)} %get-tuple-element.5.up), custom_call_target="tpu_custom_call" | custom-call | bytes 3145728 | tf_op jit(solution)/shard_map/pallas_call | solution.py:408
